TPU v7x, 512 devices: a whole 4x8x8 slice. The times are simulated.
512 devices in a mesh: dp: 32 (over y_lo, z), owner: 16 (over x, y_hi, core).
Axes of the slice: x: 4, y: 8 (y_hi: 2, y_lo: 4; y = y_hi * 4 + y_lo), z: 8, core: 2. Of those that a mesh axis runs over, the one named last changes fastest.
Arguments:
- gradients: bfloat16 [32, 16, 512, 512], P('dp', 'owner'), may hold values from -600 to 600
- block_layer: int32 [16], P('owner'), may hold values from 0 to 3
Outputs:
- update: bfloat16 [16, 512, 512], P('owner', 'dp')
All inputs are finite; a program needn't handle non-finite values.
Results may differ from a plain program's by a relative error of at most 0.0062.
Values may be sent and summed in bfloat16 or wider, within the bound.
No kernel may reach another device: no remote copies, remote signals or barrier semaphores. Data moves between devices by JAX's collectives and lax.ppermute only.
A program may use at most 64 MiB of HBM per device.

v0:
```python
import jax
import jax.numpy as jnp
from jax import lax
from jax.sharding import Mesh
from jax.sharding import PartitionSpec as P

LAYERS = 4
ITERS = 3
DP = ("dp_0", "dp_1")
DP_OWNER = ("dp_0", "dp_1", "owner_0", "owner_1", "owner_2")
OWNER = ("owner_0", "owner_1", "owner_2")


def from_partner(x, axis, distance):
    return lax.ppermute(x, axis, [(i, i ^ 1 << distance) for i in range(lax.axis_size(axis))])


def cut_along(x, dim, size):
    lengths = x.shape
    parts = x.reshape(*lengths[:dim], size, lengths[dim] // size, *lengths[dim + 1 :])
    return jnp.moveaxis(parts, dim, 0)


def summed_on_arrival(x, axis, dim):
    parts = cut_along(x, dim, lax.axis_size(axis))
    arrived = lax.all_to_all(parts, axis, split_axis=0, concat_axis=0, tiled=True)
    return arrived.sum(axis=0)


def sent_to_all(x, axis):
    size = lax.axis_size(axis)
    return lax.all_to_all(jnp.broadcast_to(x[None], (size, *x.shape)), axis, 0, 0, tiled=True)


def laid_out(parts, dim):
    lengths = list(parts.shape[1:])
    lengths[dim] *= parts.shape[0]
    return jnp.moveaxis(parts, 0, dim).reshape(lengths)


def gathered_copies(x, axis, dim):
    parts = sent_to_all(x, axis)
    return laid_out(parts, dim)


def by_axis(x, axes):
    for axis in axes:
        x = lax.psum(x, axis)
    return x


def own_whole(partial_rows, position, members):
    gathered = partial_rows
    for bit_number in range(members.bit_length() - 1):
        partner = from_partner(gathered, DP, bit_number)
        upper_half = position // (1 << bit_number) % 2 == 1
        gathered = jnp.where(
            upper_half,
            jnp.concatenate([partner, gathered], axis=0),
            jnp.concatenate([gathered, partner], axis=0),
        )
    return gathered


def keep_whole(partial_rows):
    return partial_rows


def root_slab(stat_rows, eye_rows, assemble):
    size_b = stat_rows.shape[1]
    identity = jnp.eye(size_b, dtype=jnp.float32)
    statistic = assemble(stat_rows)
    ridge_term = 0.01 * jnp.trace(statistic) / size_b + 1e-06
    shifted_whole = statistic + ridge_term * identity
    scaling = jnp.sqrt(jnp.sum(shifted_whole * shifted_whole))
    current_whole = shifted_whole / scaling
    current_rows = (stat_rows + ridge_term * eye_rows) / scaling
    inverse_rows = eye_rows
    for step_number in range(ITERS):
        factor_whole = (5.0 * identity - current_whole) / 4.0
        factor_rows = (5.0 * eye_rows - current_rows) / 4.0
        if step_number == 0:
            inverse_rows = scaling ** (-0.25) * factor_rows
        else:
            inverse_rows = jnp.dot(inverse_rows, factor_whole, precision=lax.Precision.HIGHEST)
        if step_number + 1 < ITERS:
            square_rows = jnp.dot(factor_rows, factor_whole, precision=lax.Precision.HIGHEST)
            square_whole = assemble(square_rows)
            fourth_rows = jnp.dot(square_rows, square_whole, precision=lax.Precision.HIGHEST)
            current_rows = jnp.dot(fourth_rows, current_whole, precision=lax.Precision.HIGHEST)
            current_whole = assemble(current_rows)
    return inverse_rows


def per_device(gradients, block_layer):
    gradient = gradients[0, 0]
    size_b = gradient.shape[0]
    dp_count = lax.axis_size(DP)
    members = dp_count // 2
    height = size_b // members
    position = lax.axis_index(DP)
    offset = position % members * height
    left_gram = lax.dot_general(
        gradient, gradient, (((1,), (1,)), ((), ())), preferred_element_type=jnp.float32
    )
    right_gram = lax.dot_general(
        gradient, gradient, (((0,), (0,)), ((), ())), preferred_element_type=jnp.float32
    )
    stacked = jnp.concatenate([left_gram, right_gram], axis=0)
    half_rows = summed_on_arrival(stacked, DP, 0)
    statistic = own_whole(half_rows, position, members)
    inverse_whole = root_slab(statistic, jnp.eye(size_b, dtype=jnp.float32), keep_whole)
    inverse_rows = lax.dynamic_slice_in_dim(inverse_whole, offset, height, 0)
    both_roots = gathered_copies(inverse_rows.astype(jnp.bfloat16), DP, 0)
    left_root = both_roots[:size_b]
    right_root = both_roots[size_b:]
    out_height = size_b // dp_count
    right_wide = right_root.astype(jnp.float32)
    left_part = lax.slice_in_dim(left_root, 0, out_height * lax.axis_size(DP), axis=0)
    middle = jnp.dot(left_part, gradient, preferred_element_type=jnp.float32)
    summed = summed_on_arrival(jnp.dot(middle, right_wide, precision=lax.Precision.HIGHEST), DP, 0)
    precond = summed / dp_count
    layer_id = block_layer[0]
    selector = (jnp.arange(LAYERS, dtype=jnp.int32) == layer_id).astype(jnp.float32)
    energy = jnp.sum(precond * precond)
    totals_sq, counts = (
        by_axis(selector * energy, DP_OWNER),
        by_axis(selector * float(precond.size), DP_OWNER),
    )
    mean_square = jnp.sum(selector * totals_sq) / jnp.sum(selector * counts)
    update = (precond * lax.rsqrt(mean_square + 1e-06)).astype(jnp.bfloat16)
    return update[None]


def solution(mesh):
    finer = Mesh(
        mesh.devices.reshape(4, 8, 4, 2, 2), ("dp_0", "dp_1", "owner_0", "owner_1", "owner_2")
    )
    in_specs = (P(DP, OWNER, None, None), P(OWNER))
    out_specs = P(OWNER, DP, None)
    return jax.shard_map(
        per_device, mesh=finer, in_specs=in_specs, out_specs=out_specs, check_vma=False
    )
```

profile of v0, /device:TPU:1, one launch (start us, length us, event | category | flops | bytes accessed | tf_op | source)
XLA Modules:
  0.0 257.0 jit_solution(7543262102058566053)
XLA Ops:
  0.0 1.0 copy-done
  2.2 62.1 %all_to_all.15 = f32[32,32,512]{2,1,0:T(8,128)S(1)} all-to-all(f32[32,32,512]{2,1,0:T(8,128)S(1)} %bitcast.32), channel_id=1, replica_groups=mesh['dp_0'=4,'dp_1'=8,'owner_0'=4,'owner_1'=2,'owner_2'=2] {'dp_0','dp_1'}, dimensions={0} | all-to-all | bytes 4194304 | tf_op jit(solution)/shard_map/all_to_all | solution.py:26
  64.4 4.5 %collective-permute-start = (f32[32,512]{1,0:T(8,128)S(1)}, f32[32,512]{1,0:T(8,128)S(1)}, u32[]{:S(2)}, u32[]{:S(2)}) collective-permute-start(f32[32,512]{1,0:T(8,128)S(1)} %reduce_sum.64), channel_id=1, source_target_pairs={{0,16},{16,0},{32,48},{48,32},{64,80},{80,64},{96,112},{112,96},{1... | collective-permute-start | bytes 196616 | tf_op jit(solution)/shard_map/ppermute | solution.py:15
  68.9 1.6 collective-permute-done
  70.6 4.3 %collective-permute-start.1 = (f32[64,512]{1,0:T(8,128)S(1)}, f32[64,512]{1,0:T(8,128)S(1)}, u32[]{:S(2)}, u32[]{:S(2)}) collective-permute-start(f32[64,512]{1,0:T(8,128)S(1)} %maximum_select_fusion.3), channel_id=1, source_target_pairs={{0,32},{16,48},{32,0},{48,16},{64,96},{80,112},{96,64},{112,80},{1... | collective-permute-start | bytes 393224 | tf_op jit(solution)/shard_map/ppermute | solution.py:15
  74.9 3.7 %collective-permute-done.1 = f32[64,512]{1,0:T(8,128)S(1)} collective-permute-done((f32[64,512]{1,0:T(8,128)S(1)}, f32[64,512]{1,0:T(8,128)S(1)}, u32[]{:S(2)}, u32[]{:S(2)}) %collective-permute-start.1) | collective-permute-done | bytes 131104 | tf_op jit(solution)/shard_map/ppermute | solution.py:15
  78.7 5.4 %collective-permute-start.2 = (f32[128,512]{1,0:T(8,128)S(1)}, f32[128,512]{1,0:T(8,128)S(1)}, u32[]{:S(2)}, u32[]{:S(2)}) collective-permute-start(f32[128,512]{1,0:T(8,128)S(1)} %maximum_select_fusion.2), channel_id=1, source_target_pairs={{0,64},{16,80},{32,96},{48,112},{64,0},{80,16},{96,32},{112,48},{1... | collective-permute-start | bytes 786440 | tf_op jit(solution)/shard_map/ppermute | solution.py:15
  84.1 12.8 %collective-permute-done.2 = f32[128,512]{1,0:T(8,128)S(1)} collective-permute-done((f32[128,512]{1,0:T(8,128)S(1)}, f32[128,512]{1,0:T(8,128)S(1)}, u32[]{:S(2)}, u32[]{:S(2)}) %collective-permute-start.2) | collective-permute-done | bytes 262176 | tf_op jit(solution)/shard_map/ppermute | solution.py:15
  96.9 1.9 collective-permute-start.3
  98.9 11.8 %collective-permute-done.3 = f32[256,512]{1,0:T(8,128)S(1)} collective-permute-done((f32[256,512]{1,0:T(8,128)S(1)}, f32[256,512]{1,0:T(8,128)S(1)}, u32[]{:S(2)}, u32[]{:S(2)}) %collective-permute-start.3) | collective-permute-done | bytes 524320 | tf_op jit(solution)/shard_map/ppermute | solution.py:15
  110.7 0.7 select_reduce_fusion
  112.0 0.9 multiply_reduce_fusion
  113.6 2.1 fusion.2
  115.7 2.8 %fusion.43 = f32[512,512]{1,0:T(8,128)} fusion(f32[512,512]{1,0:T(8,128)S(1)} %fusion.2), kind=kOutput, calls=%fused_computation.56 | convolution fusion | flops 1610612736 | bytes 2097152 | tf_op jit(solution)/shard_map/dot_general | solution.py:89
  118.6 3.2 %fusion.39 = f32[512,512]{1,0:T(8,128)S(1)} fusion(f32[512,512]{1,0:T(8,128)} %fusion.43, f32[]{:T(128)S(6)} %sqrt.3, f32[]{:T(128)S(6)} %add.61, f32[256,512]{1,0:T(8,128)S(1)} %collective-permute-done.3, f32[256,512]{1,0:T(8,128)S(1)} %maximum_select_fusion.1, pred[]{:T(512)S(6)} %eq.39), kind=kOutput, calls=%fused_computation.54 | convolution fusion | flops 1612447744 | bytes 3145737 | tf_op jit(solution)/shard_map/dot_general | solution.py:90
  121.8 1.9 fusion.7
  123.7 1.8 fusion.44
  125.5 1.9 fusion
  127.4 3.3 %fusion.4 = f32[512,512]{1,0:T(8,128)S(1)} fusion(f32[512,512]{1,0:T(8,128)S(1)} %fusion.39, f32[]{:T(128)S(6)} %mul.75, f32[]{:T(128)S(6)} %sqrt.3, f32[]{:T(128)S(6)} %add.61, f32[256,512]{1,0:T(8,128)} %copy-done.1, f32[256,512]{1,0:T(8,128)S(1)} %maximum_select_fusion.1, pred[]{:T(512)S(6)} %eq.39), kind=kOutput, calls=%fused_computation.9 | convolution fusion | flops 1614282752 | bytes 3145741 | tf_op jit(solution)/shard_map/dot_general | solution.py:85
  130.7 2.0 fusion.45
  132.9 32.6 %all_to_all.16 = bf16[32,32,512]{2,1,0:T(8,128)(2,1)S(1)} all-to-all(bf16[32,32,512]{2,1,0:T(8,128)(2,1)S(1)} %broadcast_in_dim.4), channel_id=1, replica_groups=mesh['dp_0'=4,'dp_1'=8,'owner_0'=4,'owner_1'=2,'owner_2'=2] {'dp_0','dp_1'}, dimensions={0} | all-to-all | bytes 2097152 | tf_op jit(solution)/shard_map/all_to_all | solution.py:32
  166.0 2.0 fusion.46
  168.0 8.0 %all-to-all-start.2 = ((f32[32,16,512]{2,1,0:T(8,128)}), f32[32,16,512]{2,1,0:T(8,128)S(1)}, u32[]{:S(2)}, u32[]{:S(2)}) async-start(f32[32,16,512]{2,1,0:T(8,128)} %fusion.46), calls=%async_computation.2 | async-start | bytes 2097152 | tf_op jit(solution)/shard_map/all_to_all | solution.py:26
  176.6 25.2 %all-to-all-done.2 = f32[32,16,512]{2,1,0:T(8,128)S(1)} async-done(((f32[32,16,512]{2,1,0:T(8,128)}), f32[32,16,512]{2,1,0:T(8,128)S(1)}, u32[]{:S(2)}, u32[]{:S(2)}) %all-to-all-start.2) | async-done | bytes 1048608 | tf_op jit(solution)/shard_map/all_to_all | solution.py:26
  202.5 0.6 fusion.28
  203.1 10.3 %all-reduce.2 = (f32[4]{0:T(128)S(1)}, f32[4]{0:T(128)S(1)}) all-reduce(f32[4]{0:T(128)S(1)} %fusion.28, f32[4]{0:T(128)S(1)} %fusion.27), channel_id=1, replica_groups=mesh['dp_0'=4,'dp_1'=8,'owner_0'=4,'owner_1'=2,'owner_2'=2] {'dp_0'}, use_global_device_ids=true, to_apply=%region_5.6 | all-reduce | flops 8 | bytes 64 | tf_op jit(solution)/shard_map/psum | solution.py:48
  213.4 13.0 %all-reduce = (f32[4]{0:T(128)S(1)}, f32[4]{0:T(128)S(1)}) all-reduce(f32[4]{0:T(128)S(1)} %get-tuple-element.9, f32[4]{0:T(128)S(1)} %get-tuple-element.10), channel_id=1, replica_groups=mesh['dp_0'=4,'dp_1'=8,'owner_0'=4,'owner_1'=2,'owner_2'=2] {'dp_1'}, use_global_device_ids=true, to_apply=%region_6.7 | all-reduce | flops 8 | bytes 64 | tf_op jit(solution)/shard_map/psum | solution.py:48
  226.4 8.9 %all-reduce.1 = (f32[4]{0:T(128)S(1)}, f32[4]{0:T(128)S(1)}) all-reduce(f32[4]{0:T(128)S(1)} %get-tuple-element.5, f32[4]{0:T(128)S(1)} %get-tuple-element.6), channel_id=1, replica_groups=mesh['dp_0'=4,'dp_1'=8,'owner_0'=4,'owner_1'=2,'owner_2'=2] {'owner_0'}, use_global_device_ids=true, to_apply=%region_7.8 | all-reduce | flops 8 | bytes 64 | tf_op jit(solution)/shard_map/psum | solution.py:48
  235.3 7.7 %all-reduce.4 = (f32[4]{0:T(128)S(1)}, f32[4]{0:T(128)S(1)}) all-reduce(f32[4]{0:T(128)S(1)} %get-tuple-element.7, f32[4]{0:T(128)S(1)} %get-tuple-element.8), channel_id=1, replica_groups=mesh['dp_0'=4,'dp_1'=8,'owner_0'=4,'owner_1'=2,'owner_2'=2] {'owner_1'}, use_global_device_ids=true, to_apply=%region_8.9 | all-reduce | flops 8 | bytes 64 | tf_op jit(solution)/shard_map/psum | solution.py:48
  243.0 11.3 %all-reduce.3 = (f32[4]{0:T(128)S(1)}, f32[4]{0:T(128)S(1)}) all-reduce(f32[4]{0:T(128)S(1)} %get-tuple-element.13, f32[4]{0:T(128)S(1)} %get-tuple-element.14), channel_id=1, replica_groups=mesh['dp_0'=4,'dp_1'=8,'owner_0'=4,'owner_1'=2,'owner_2'=2] {'owner_2'}, use_global_device_ids=true, to_apply=%region_9.10 | all-reduce | flops 8 | bytes 64 | tf_op jit(solution)/shard_map/psum | solution.py:48
  254.3 0.7 select_reduce_fusion.1
  256.4 0.6 fusion.26
  (17 shorter events, 2.7 us)
Async XLA Ops:
  0.0 1.0 copy-start
  64.4 6.1 %collective-permute-start = (f32[32,512]{1,0:T(8,128)S(1)}, f32[32,512]{1,0:T(8,128)S(1)}, u32[]{:S(2)}, u32[]{:S(2)}) collective-permute-start(f32[32,512]{1,0:T(8,128)S(1)} %reduce_sum.64), channel_id=1, source_target_pairs={{0,16},{16,0},{32,48},{48,32},{64,80},{80,64},{96,112},{112,96},{1... | collective-permute-start | bytes 196616 | tf_op jit(solution)/shard_map/ppermute | solution.py:15
  70.6 8.1 %collective-permute-start.1 = (f32[64,512]{1,0:T(8,128)S(1)}, f32[64,512]{1,0:T(8,128)S(1)}, u32[]{:S(2)}, u32[]{:S(2)}) collective-permute-start(f32[64,512]{1,0:T(8,128)S(1)} %maximum_select_fusion.3), channel_id=1, source_target_pairs={{0,32},{16,48},{32,0},{48,16},{64,96},{80,112},{96,64},{112,80},{1... | collective-permute-start | bytes 393224 | tf_op jit(solution)/shard_map/ppermute | solution.py:15
  78.7 18.2 %collective-permute-start.2 = (f32[128,512]{1,0:T(8,128)S(1)}, f32[128,512]{1,0:T(8,128)S(1)}, u32[]{:S(2)}, u32[]{:S(2)}) collective-permute-start(f32[128,512]{1,0:T(8,128)S(1)} %maximum_select_fusion.2), channel_id=1, source_target_pairs={{0,64},{16,80},{32,96},{48,112},{64,0},{80,16},{96,32},{112,48},{1... | collective-permute-start | bytes 786440 | tf_op jit(solution)/shard_map/ppermute | solution.py:15
  96.9 13.8 %collective-permute-start.3 = (f32[256,512]{1,0:T(8,128)S(1)}, f32[256,512]{1,0:T(8,128)S(1)}, u32[]{:S(2)}, u32[]{:S(2)}) collective-permute-start(f32[256,512]{1,0:T(8,128)S(1)} %maximum_select_fusion.1), channel_id=1, source_target_pairs={{0,128},{16,144},{32,160},{48,176},{64,192},{80,208},{96,224},{112... | collective-permute-start | bytes 1572872 | tf_op jit(solution)/shard_map/ppermute | solution.py:15
  110.7 7.9 %copy-start.1 = (f32[256,512]{1,0:T(8,128)}, f32[256,512]{1,0:T(8,128)S(1)}, u32[]{:S(2)}) copy-start(f32[256,512]{1,0:T(8,128)S(1)} %collective-permute-done.3) | copy-start | bytes 1572868
  168.0 33.8 %all-to-all-start.2 = ((f32[32,16,512]{2,1,0:T(8,128)}), f32[32,16,512]{2,1,0:T(8,128)S(1)}, u32[]{:S(2)}, u32[]{:S(2)}) async-start(f32[32,16,512]{2,1,0:T(8,128)} %fusion.46), calls=%async_computation.2 | async-start | bytes 2097152 | tf_op jit(solution)/shard_map/all_to_all | solution.py:26
where the time goes:
time: 258 us; the launch traced here: 257 us
  blocking collectives  146 us (57%)
  waiting for transfers between devices  55.1 us (21%)
  starting transfers between devices  24.1 us (9%)
  matrix products  22.3 us (9%)
  other arithmetic  4.59 us (2%)
  between operations  3.79 us (1%)
    all_to_all x1, blocking collectives, summed_on_arrival(): lax.all_to_all(parts, axis, split_axis=0, concat_axis=0, tiled=True)  62.1 us
    psum x5, blocking collectives, by_axis(): x = lax.psum(x, axis)  51.1 us
    all_to_all x1, blocking collectives, sent_to_all(): lax.all_to_all(jnp.broadcast_to(x[None], (size, *x.shape)), axis, 0, 0, t...  32.6 us
    ppermute x4, waiting for transfers between devices, from_partner(): lax.ppermute(x, axis, [(i, i ^ 1 << distance) for i in range(lax.axis_siz...  29.9 us
    all_to_all x1, waiting for transfers between devices, summed_on_arrival(): lax.all_to_all(parts, axis, split_axis=0, concat_axis=0, tiled=True)  25.2 us
    ppermute x4, starting transfers between devices, from_partner(): lax.ppermute(x, axis, [(i, i ^ 1 << distance) for i in range(lax.axis_siz...  16.1 us
    all_to_all x1, starting transfers between devices, summed_on_arrival(): lax.all_to_all(parts, axis, split_axis=0, concat_axis=0, tiled=True)  7.95 us
    dot_general x2, matrix products, root_slab(): jnp.dot(inverse_rows, factor_whole, precision=lax.Precision.HIGHEST)  5.3 us
  transfers between devices with their start and end apart: 5, of which 5 were waited for; matrix products, arithmetic and copies ran while one was open for 0% of the time, Pallas kernels for 0%

commit v1 on v0

--- a/solution.py
+++ b/solution.py
@@ -9,6 +9,12 @@
 DP = ("dp_0", "dp_1")
 DP_OWNER = ("dp_0", "dp_1", "owner_0", "owner_1", "owner_2")
 OWNER = ("owner_0", "owner_1", "owner_2")
+
+
+def summed_here(x, mesh_axis):
+    parts = lax.all_gather(x, mesh_axis, axis=0, tiled=False)
+    acc = parts.sum(axis=0)
+    return acc
 
 
 def from_partner(x, axis, distance):
@@ -45,7 +51,7 @@
 
 def by_axis(x, axes):
     for axis in axes:
-        x = lax.psum(x, axis)
+        x = summed_here(x, axis)
     return x
 
 

time: 258 us -> 274 us (1.062)
  blocking collectives: 146 us -> 114 us
  waiting for transfers between devices: 55.1 us -> 80.2 us
  starting transfers between devices: 24.1 us -> 35.1 us
  local copies, waits for them, and re-layouts: 1.27 us -> 8.85 us
    all_to_all x1 -> x0, blocking collectives: 62.1 us -> none  [summed_on_arrival(): lax.all_to_all(parts, axis, split_axis=0, concat_axis=0, tiled=True)]
    psum x5 -> x0, blocking collectives: 51.1 us -> none  [by_axis(): x = lax.psum(x, axis)]
    unnamed x0 -> x4, blocking collectives: none -> 45.4 us
    all_gather x0 -> x2, blocking collectives: none -> 33.5 us  [summed_here(): parts = lax.all_gather(x, mesh_axis, axis=0, tiled=False)]
    all_to_all x1 -> x2, waiting for transfers between devices: 25.2 us -> 54.4 us  [summed_on_arrival(): lax.all_to_all(parts, axis, split_axis=0, concat_axis=0, tiled=True)]
    all_to_all x1 -> x2, starting transfers between devices: 7.95 us -> 22.3 us  [summed_on_arrival(): lax.all_to_all(parts, axis, split_axis=0, concat_axis=0, tiled=True)]
    unnamed x4 -> x24, local copies, waits for them, and re-layouts: 1.05 us -> 7.97 us
    ppermute x4, waiting for transfers between devices: 29.9 us -> 25.8 us  [from_partner(): lax.ppermute(x, axis, [(i, i ^ 1 << distance) for i in range(lax.axis_siz...]
  transfers between devices with their start and end apart: 5 -> 6, of which waited for: 5 -> 5; matrix products, arithmetic and copies ran while one was open for 0% -> 2% of each run, Pallas kernels for 0% -> 0%
where the time goes in v1:
time: 274 us; the launch traced here: 273 us
  blocking collectives  114 us (42%)
  waiting for transfers between devices  80.2 us (29%)
  starting transfers between devices  35.1 us (13%)
  matrix products  22.3 us (8%)
  local copies, waits for them, and re-layouts  8.85 us (3%)
  between operations  6.34 us (2%)
  other arithmetic  6.14 us (2%)
    all_to_all x2, waiting for transfers between devices, summed_on_arrival(): lax.all_to_all(parts, axis, split_axis=0, concat_axis=0, tiled=True)  54.4 us
    unnamed x4, blocking collectives  45.4 us
    all_to_all x1, blocking collectives, sent_to_all(): lax.all_to_all(jnp.broadcast_to(x[None], (size, *x.shape)), axis, 0, 0, t...  35.6 us
    all_gather x2, blocking collectives, summed_here(): parts = lax.all_gather(x, mesh_axis, axis=0, tiled=False)  33.5 us
    ppermute x4, waiting for transfers between devices, from_partner(): lax.ppermute(x, axis, [(i, i ^ 1 << distance) for i in range(lax.axis_siz...  25.8 us
    all_to_all x2, starting transfers between devices, summed_on_arrival(): lax.all_to_all(parts, axis, split_axis=0, concat_axis=0, tiled=True)  22.3 us
    ppermute x4, starting transfers between devices, from_partner(): lax.ppermute(x, axis, [(i, i ^ 1 << distance) for i in range(lax.axis_siz...  12.8 us
    unnamed x24, local copies, waits for them, and re-layouts  7.97 us
  transfers between devices with their start and end apart: 6, of which 5 were waited for; matrix products, arithmetic and copies ran while one was open for 2% of the time, Pallas kernels for 0%

profile of v1, /device:TPU:1, one launch (start us, length us, event | category | flops | bytes accessed | tf_op | source)
XLA Modules:
  0.0 273.4 jit_solution(2825666327140643382)
XLA Ops:
  2.0 1.5 pad_maximum_fusion
  3.5 14.3 %all-to-all-start = ((f32[32,32,512]{2,1,0:T(8,128)}), f32[32,32,512]{2,1,0:T(8,128)S(1)}, u32[]{:S(2)}, u32[]{:S(2)}) async-start(f32[32,32,512]{2,1,0:T(8,128)} %bitcast.40), calls=%async_computation | async-start | bytes 4194304 | tf_op jit(solution)/shard_map/all_to_all | solution.py:32
  17.8 54.4 %all-to-all-done = f32[32,32,512]{2,1,0:T(8,128)S(1)} async-done(((f32[32,32,512]{2,1,0:T(8,128)}), f32[32,32,512]{2,1,0:T(8,128)S(1)}, u32[]{:S(2)}, u32[]{:S(2)}) %all-to-all-start) | async-done | bytes 2097184 | tf_op jit(solution)/shard_map/all_to_all | solution.py:32
  72.3 2.0 collective-permute-start
  74.4 2.9 %collective-permute-done = f32[32,512]{1,0:T(8,128)S(1)} collective-permute-done((f32[32,512]{1,0:T(8,128)S(1)}, f32[32,512]{1,0:T(8,128)S(1)}, u32[]{:S(2)}, u32[]{:S(2)}) %collective-permute-start) | collective-permute-done | bytes 65568 | tf_op jit(solution)/shard_map/ppermute | solution.py:21
  77.3 2.0 collective-permute-start.1
  79.4 5.8 %collective-permute-done.1 = f32[64,512]{1,0:T(8,128)S(1)} collective-permute-done((f32[64,512]{1,0:T(8,128)S(1)}, f32[64,512]{1,0:T(8,128)S(1)}, u32[]{:S(2)}, u32[]{:S(2)}) %collective-permute-start.1) | collective-permute-done | bytes 131104 | tf_op jit(solution)/shard_map/ppermute | solution.py:21
  85.2 6.1 %collective-permute-start.2 = (f32[128,512]{1,0:T(8,128)S(1)}, f32[128,512]{1,0:T(8,128)S(1)}, u32[]{:S(2)}, u32[]{:S(2)}) collective-permute-start(f32[128,512]{1,0:T(8,128)S(1)} %maximum_select_fusion.2), channel_id=1, source_target_pairs={{0,64},{16,80},{32,96},{48,112},{64,0},{80,16},{96,32},{112,48},{1... | collective-permute-start | bytes 786440 | tf_op jit(solution)/shard_map/ppermute | solution.py:21
  91.3 8.7 %collective-permute-done.2 = f32[128,512]{1,0:T(8,128)S(1)} collective-permute-done((f32[128,512]{1,0:T(8,128)S(1)}, f32[128,512]{1,0:T(8,128)S(1)}, u32[]{:S(2)}, u32[]{:S(2)}) %collective-permute-start.2) | collective-permute-done | bytes 262176 | tf_op jit(solution)/shard_map/ppermute | solution.py:21
  100.1 2.6 collective-permute-start.3
  102.8 8.3 %collective-permute-done.3 = f32[256,512]{1,0:T(8,128)S(1)} collective-permute-done((f32[256,512]{1,0:T(8,128)S(1)}, f32[256,512]{1,0:T(8,128)S(1)}, u32[]{:S(2)}, u32[]{:S(2)}) %collective-permute-start.3) | collective-permute-done | bytes 524320 | tf_op jit(solution)/shard_map/ppermute | solution.py:21
  114.1 2.1 fusion.2
  116.1 2.8 %fusion.45 = f32[512,512]{1,0:T(8,128)} fusion(f32[512,512]{1,0:T(8,128)S(1)} %fusion.2), kind=kOutput, calls=%fused_computation.59 | convolution fusion | flops 1610612736 | bytes 2097152 | tf_op jit(solution)/shard_map/dot_general | solution.py:95
  119.1 3.2 %fusion.41 = f32[512,512]{1,0:T(8,128)S(1)} fusion(f32[512,512]{1,0:T(8,128)} %fusion.45, f32[]{:T(128)S(6)} %sqrt.3, f32[]{:T(128)S(6)} %add.41, f32[256,512]{1,0:T(8,128)S(1)} %collective-permute-done.3, f32[256,512]{1,0:T(8,128)S(1)} %maximum_select_fusion.1, pred[]{:T(512)S(6)} %eq.54), kind=kOutput, calls=%fused_computation.57 | convolution fusion | flops 1612447744 | bytes 3145737 | tf_op jit(solution)/shard_map/dot_general | solution.py:96
  122.2 1.9 fusion.7
  124.1 1.8 fusion.46
  126.0 1.9 fusion
  127.8 3.3 %fusion.4 = f32[512,512]{1,0:T(8,128)S(1)} fusion(f32[512,512]{1,0:T(8,128)S(1)} %fusion.41, f32[]{:T(128)S(6)} %mul.75, f32[]{:T(128)S(6)} %sqrt.3, f32[]{:T(128)S(6)} %add.41, f32[256,512]{1,0:T(8,128)} %copy-done.1, f32[256,512]{1,0:T(8,128)S(1)} %maximum_select_fusion.1, pred[]{:T(512)S(6)} %eq.54), kind=kOutput, calls=%fused_computation.9 | convolution fusion | flops 1614282752 | bytes 3145741 | tf_op jit(solution)/shard_map/dot_general | solution.py:91
  131.1 2.0 fusion.47
  133.3 35.6 %all_to_all.15 = bf16[32,32,512]{2,1,0:T(8,128)(2,1)S(1)} all-to-all(bf16[32,32,512]{2,1,0:T(8,128)(2,1)S(1)} %broadcast_in_dim.4), channel_id=1, replica_groups=mesh['dp_0'=4,'dp_1'=8,'owner_0'=4,'owner_1'=2,'owner_2'=2] {'dp_0','dp_1'}, dimensions={0} | all-to-all | bytes 2097152 | tf_op jit(solution)/shard_map/all_to_all | solution.py:38
  169.4 2.0 fusion.48
  171.4 8.0 %all-to-all-start.2 = ((f32[32,16,512]{2,1,0:T(8,128)}), f32[32,16,512]{2,1,0:T(8,128)S(1)}, u32[]{:S(2)}, u32[]{:S(2)}) async-start(f32[32,16,512]{2,1,0:T(8,128)} %fusion.48), calls=%async_computation.2 | async-start | bytes 2097152 | tf_op jit(solution)/shard_map/all_to_all | solution.py:32
  180.1 22.2 %all-gather.9 = f32[4,1,4]{2,1,0:T(1,128)S(1)} all-gather(f32[1,1,4]{2,1,0:T(1,128)S(1)} %fusion.28), channel_id=1, replica_groups=mesh['dp_0'=4,'dp_1'=8,'owner_0'=4,'owner_1'=2,'owner_2'=2] {'dp_0'}, dimensions={0}, use_global_device_ids=true | all-gather | bytes 80 | tf_op jit(solution)/shard_map/all_gather | solution.py:15
  202.3 1.3 dynamic-slice
  203.6 1.2 dynamic-slice.1
  206.0 1.3 dynamic-slice.2
  208.0 1.3 dynamic-slice.3
  210.9 11.3 %all-gather.8 = f32[4,1,4]{2,1,0:T(1,128)S(1)} all-gather(f32[1,1,4]{2,1,0:T(1,128)S(1)} %fusion.27), channel_id=1, replica_groups=mesh['dp_0'=4,'dp_1'=8,'owner_0'=4,'owner_1'=2,'owner_2'=2] {'dp_0'}, dimensions={0}, use_global_device_ids=true | all-gather | bytes 80 | tf_op jit(solution)/shard_map/all_gather | solution.py:15
  222.4 13.0 %all-reduce.8 = (f32[32]{0:T(128)S(1)}, f32[32]{0:T(128)S(1)}) all-reduce(f32[32]{0:T(128)S(1)} %dynamic-update-slice, f32[32]{0:T(128)S(1)} %dynamic-update-slice.4), channel_id=2, replica_groups=mesh['dp_0'=4,'dp_1'=8,'owner_0'=4,'owner_1'=2,'owner_2'=2] {'dp_1'}, use_global_device_ids=true, to_apply=%add | all-reduce | flops 64 | bytes 512
  236.1 10.4 %all-reduce.9 = (f32[16]{0:T(128)S(1)}, f32[16]{0:T(128)S(1)}) all-reduce(f32[16]{0:T(128)S(1)} %dynamic-update-slice.1, f32[16]{0:T(128)S(1)} %dynamic-update-slice.5), channel_id=3, replica_groups=mesh['dp_0'=4,'dp_1'=8,'owner_0'=4,'owner_1'=2,'owner_2'=2] {'owner_0'}, use_global_device_ids=true, to_apply=%add.1 | all-reduce | flops 32 | bytes 256
  247.9 9.8 %all-reduce.11 = (f32[8]{0:T(128)S(1)}, f32[8]{0:T(128)S(1)}) all-reduce(f32[8]{0:T(128)S(1)} %dynamic-update-slice.2, f32[8]{0:T(128)S(1)} %dynamic-update-slice.6), channel_id=4, replica_groups=mesh['dp_0'=4,'dp_1'=8,'owner_0'=4,'owner_1'=2,'owner_2'=2] {'owner_1'}, use_global_device_ids=true, to_apply=%add.2 | all-reduce | flops 16 | bytes 128
  258.3 12.1 %all-reduce.10 = (f32[8]{0:T(128)S(1)}, f32[8]{0:T(128)S(1)}) all-reduce(f32[8]{0:T(128)S(1)} %dynamic-update-slice.3, f32[8]{0:T(128)S(1)} %dynamic-update-slice.7), channel_id=5, replica_groups=mesh['dp_0'=4,'dp_1'=8,'owner_0'=4,'owner_1'=2,'owner_2'=2] {'owner_2'}, use_global_device_ids=true, to_apply=%add.3 | all-reduce | flops 16 | bytes 128
  (57 shorter events, 9.7 us)
Async XLA Ops:
  0.0 1.0 copy-start
  3.5 68.7 %all-to-all-start = ((f32[32,32,512]{2,1,0:T(8,128)}), f32[32,32,512]{2,1,0:T(8,128)S(1)}, u32[]{:S(2)}, u32[]{:S(2)}) async-start(f32[32,32,512]{2,1,0:T(8,128)} %bitcast.40), calls=%async_computation | async-start | bytes 4194304 | tf_op jit(solution)/shard_map/all_to_all | solution.py:32
  72.3 5.0 %collective-permute-start = (f32[32,512]{1,0:T(8,128)S(1)}, f32[32,512]{1,0:T(8,128)S(1)}, u32[]{:S(2)}, u32[]{:S(2)}) collective-permute-start(f32[32,512]{1,0:T(8,128)S(1)} %reduce_sum.154), channel_id=1, source_target_pairs={{0,16},{16,0},{32,48},{48,32},{64,80},{80,64},{96,112},{112,96},{1... | collective-permute-start | bytes 196616 | tf_op jit(solution)/shard_map/ppermute | solution.py:21
  77.3 7.9 %collective-permute-start.1 = (f32[64,512]{1,0:T(8,128)S(1)}, f32[64,512]{1,0:T(8,128)S(1)}, u32[]{:S(2)}, u32[]{:S(2)}) collective-permute-start(f32[64,512]{1,0:T(8,128)S(1)} %maximum_select_fusion.3), channel_id=1, source_target_pairs={{0,32},{16,48},{32,0},{48,16},{64,96},{80,112},{96,64},{112,80},{1... | collective-permute-start | bytes 393224 | tf_op jit(solution)/shard_map/ppermute | solution.py:21
  85.2 14.8 %collective-permute-start.2 = (f32[128,512]{1,0:T(8,128)S(1)}, f32[128,512]{1,0:T(8,128)S(1)}, u32[]{:S(2)}, u32[]{:S(2)}) collective-permute-start(f32[128,512]{1,0:T(8,128)S(1)} %maximum_select_fusion.2), channel_id=1, source_target_pairs={{0,64},{16,80},{32,96},{48,112},{64,0},{80,16},{96,32},{112,48},{1... | collective-permute-start | bytes 786440 | tf_op jit(solution)/shard_map/ppermute | solution.py:21
  100.1 11.0 %collective-permute-start.3 = (f32[256,512]{1,0:T(8,128)S(1)}, f32[256,512]{1,0:T(8,128)S(1)}, u32[]{:S(2)}, u32[]{:S(2)}) collective-permute-start(f32[256,512]{1,0:T(8,128)S(1)} %maximum_select_fusion.1), channel_id=1, source_target_pairs={{0,128},{16,144},{32,160},{48,176},{64,192},{80,208},{96,224},{112... | collective-permute-start | bytes 1572872 | tf_op jit(solution)/shard_map/ppermute | solution.py:21
  111.1 7.9 %copy-start.1 = (f32[256,512]{1,0:T(8,128)}, f32[256,512]{1,0:T(8,128)S(1)}, u32[]{:S(2)}) copy-start(f32[256,512]{1,0:T(8,128)S(1)} %collective-permute-done.3) | copy-start | bytes 1572868
  171.4 37.9 %all-to-all-start.2 = ((f32[32,16,512]{2,1,0:T(8,128)}), f32[32,16,512]{2,1,0:T(8,128)S(1)}, u32[]{:S(2)}, u32[]{:S(2)}) async-start(f32[32,16,512]{2,1,0:T(8,128)} %fusion.48), calls=%async_computation.2 | async-start | bytes 2097152 | tf_op jit(solution)/shard_map/all_to_all | solution.py:32
